TPU v7x, 32 devices: a whole 2x2x4 slice. The times are simulated.
32 devices in a mesh: year: 8 (over y, x, core), port: 4 (over z).
Axes of the slice: x: 2, y: 2, z: 4, core: 2. Of those that a mesh axis runs over, the one named last changes fastest.
Arguments:
- event_loss: bfloat16 [4096, 4096], P('year', 'port'), may hold values from 0 to 24
- event_year: int32 [4096], P('year'), may hold values from -1 to 255, as said below
- retention: float32 [4096], P('port'), may hold values from 0.2 to 2
- risk_limit: float32 [4096], P('port'), may hold values from 1 to 8
- cession_share: bfloat16 [4096, 4], P('port'), may hold values from 0.099609375 to 1
- member_treaty: int32 [4096, 4], P('port'), may hold values from 0 to 1023, all different within a row
- attach_tier: int32 [1024], P('port'), may hold values from 2 to 11
- limit_tier: int32 [1024], P('port'), may hold values from 2 to 10
- reinstatements: int32 [1024], P('port'), may hold values from 0 to 3
- reinstate_rate: float32 [1024], P('port'), may hold values from 0.1 to 1
- stop_attach: float32 [1024], P('port'), may hold values from 0.7 to 2
- stop_width: float32 [1024], P('port'), may hold values from 0.3 to 2
Outputs:
- layer_net: float32 [1024, 256], P('port', 'year')
- stop_loss: float32 [1024, 256], P('port', 'year')
- tail_mean: float32 [1024], P('port')
Inputs may be any that keep to these rules, and one draw needn't show every extreme that they name: `event_year`: the 512 rows of year-block b name years b * 32 to (b + 1) * 32 - 1 in nondecreasing order, followed by padding rows marked -1; at least one block has no padding row. `member_treaty`: each portfolio names 4 different treaties, and every treaty is named by some portfolio.
All inputs are finite; a program needn't handle non-finite values.
Results may differ from a plain program's by a relative error of at most 0.029.
Values may be sent and summed in bfloat16 or wider, within the bound.
A program may use at most 64 MiB of HBM per device.

v0:
```python
import jax
import jax.numpy as jnp
from jax import lax
from jax.sharding import PartitionSpec as P

TREATIES = 1024
MEMB = 4
YEAR_DEV = 32
TAIL = 16
UNIT_LOSS = 1.0


def combined_all(part, axis, combine):
    gathered = lax.all_gather(part, axis)

    def take(source):
        return lax.dynamic_index_in_dim(gathered, source, 0, False)

    return lax.fori_loop(
        1, lax.axis_size(axis), lambda source, state: combine(state, take(source)), take(0)
    )


def clamp_between(values, lower, upper):
    return jnp.minimum(jnp.maximum(values, lower), upper)


def top_years(values, keep_count):
    return jnp.sort(values, axis=1)[:, values.shape[1] - keep_count :]


def on_device(
    event_loss,
    event_year,
    retention,
    risk_limit,
    cession_share,
    member_treaty,
    attach_tier,
    limit_tier,
    reinstatements,
    reinstate_rate,
    stop_attach,
    stop_width,
):
    own_count = attach_tier.shape[0]
    ceded_loss = clamp_between(
        event_loss.astype(jnp.float32) - retention[None, :], 0.0, risk_limit[None, :]
    ).astype(jnp.bfloat16)
    treaty_ids = lax.broadcasted_iota(jnp.int32, (1, TREATIES), 1)
    weights = jnp.zeros((event_loss.shape[1], TREATIES), jnp.float32)
    for member_slot in range(MEMB):
        picked = member_treaty[:, member_slot : member_slot + 1] == treaty_ids
        weights = weights + jnp.where(
            picked, cession_share[:, member_slot : member_slot + 1].astype(jnp.float32), 0.0
        )
    weights = weights.astype(jnp.bfloat16)
    first_year = lax.axis_index("year") * YEAR_DEV
    local_year = event_year - first_year
    contract = (((0,), (1,)), ((), ()))
    event_treaty = lax.psum_scatter(
        lax.dot_general(weights, ceded_loss, contract, preferred_element_type=jnp.float32).astype(
            jnp.bfloat16
        ),
        "port",
        scatter_dimension=0,
        tiled=True,
    ).astype(jnp.float32)
    attach = attach_tier.astype(jnp.float32) * UNIT_LOSS
    limit_loss = limit_tier.astype(jnp.float32) * UNIT_LOSS
    recovered = clamp_between(event_treaty - attach[:, None], 0.0, limit_loss[:, None])
    retained = event_treaty - recovered
    year_hits = (local_year[:, None] == lax.broadcasted_iota(jnp.int32, (1, YEAR_DEV), 1)).astype(
        jnp.float32
    )
    yearly = jnp.dot(
        jnp.concatenate((recovered, retained), 0),
        year_hits,
        precision=lax.Precision.HIGHEST,
        preferred_element_type=jnp.float32,
    )
    annual = yearly[:own_count]
    kept_annual = yearly[own_count:]
    reinstated = reinstatements.astype(jnp.float32)
    layer_paid = jnp.minimum(annual, ((1.0 + reinstated) * limit_loss)[:, None])
    layer_net = (
        layer_paid
        - reinstate_rate[:, None] * jnp.minimum(layer_paid, (reinstated * limit_loss)[:, None])
    ) / limit_loss[:, None]
    year_total = YEAR_DEV * lax.axis_size("year")
    summed = lax.psum(jnp.sum(kept_annual, axis=1), "year")
    base_loss = UNIT_LOSS + summed / year_total
    loss_ratio = kept_annual / base_loss[:, None]

    def keep_largest(earlier, later):
        return top_years(jnp.concatenate((earlier, later), 1), TAIL)

    largest = combined_all(top_years(loss_ratio, TAIL), "year", keep_largest)
    tail_mean = jnp.mean(largest, axis=1)
    stop_loss = clamp_between(loss_ratio - stop_attach[:, None], 0.0, stop_width[:, None])
    return (layer_net, stop_loss, tail_mean)


def solution(mesh):
    return jax.shard_map(
        on_device,
        mesh=mesh,
        in_specs=(
            P("year", "port"),
            P("year"),
            P("port"),
            P("port"),
            P("port", None),
            P("port", None),
            P("port"),
            P("port"),
            P("port"),
            P("port"),
            P("port"),
            P("port"),
        ),
        out_specs=(P("port", "year"), P("port", "year"), P("port")),
        check_vma=False,
    )
```

profile of v0, /device:TPU:0, one launch (start us, length us, event | category | flops | bytes accessed | tf_op | source)
XLA Modules:
  0.0 85.3 jit_solution(53839467080890265)
XLA Ops:
  7.2 0.0 reduce-scatter.2.cloned.1.call-start
  7.2 0.9 %fusion.23 = (s32[1024,1]{0,1:T(1,128)S(1)}, s32[1024,1]{0,1:T(1,128)S(1)}, s32[1024,1]{0,1:T(1,128)S(1)}, s32[1024,1]{0,1:T(1,128)S(1)}) fusion(s32[1024,4]{0,1:T(4,128)} %param.19), kind=kLoop, calls=%fused_computation.49 | loop fusion | bytes 32768 | tf_op jit(solution)/shard_map/slice | solution.py:53
  8.1 0.9 %slice_convert_fusion.3 = (f32[1024,1]{0,1:T(1,128)S(1)}, f32[1024,1]{0,1:T(1,128)S(1)}, f32[1024,1]{0,1:T(1,128)S(1)}, f32[1024,1]{0,1:T(1,128)S(1)}) fusion(bf16[1024,4]{0,1:T(4,128)(2,1)} %param.18), kind=kLoop, calls=%fused_computation.41 | loop fusion | flops 4096 | bytes 24576 | tf_op jit(solution)/shard_map/jit(_where)/broadcast_in_dim | solution.py:54
  9.0 5.4 %fusion.10 = bf16[1024,512]{1,0:T(8,128)(2,1)} fusion(f32[1024]{0:T(1024)S(1)} %bitcast.26, s32[1024]{0:T(1024)S(1)} %bitcast.22, f32[1024]{0:T(1024)S(1)} %bitcast.27, s32[1024]{0:T(1024)S(1)} %bitcast.23, f32[1024]{0:T(1024)S(1)} %bitcast.25, s32[1024]{0:T(1024)S(1)} %bitcast.21, f32[1024]{0:T(1024)S(1)} %bitcast.24, s32[1024]{0:T(1024)S(1)} %bitcast.20, ...), kind=kOutput, calls=%fused_computation.19 | convolution fusion | flops 1089994752 | bytes 2138112 | tf_op jit(solution)/shard_map/dot_general | solution.py:62
  14.4 0.0 copy-start
  14.4 0.0 copy-start.5
  14.4 0.0 copy-start.6
  14.4 0.0 copy-start.1
  14.4 0.0 reduce-scatter.2.cloned.1.call-update
  14.5 0.6 copy-done
  15.1 0.0 copy-done.5
  15.1 0.0 copy-done.6
  15.1 0.0 copy-done.1
  15.1 0.0 copy-start.2
  15.2 0.0 copy-start.3
  15.2 0.0 copy-start.4
  15.2 29.4 %reduce-scatter.2.cloned.1.call-done = bf16[256,512]{1,0:T(8,128)(2,1)} async-done(((bf16[1024,512]{1,0:T(8,128)(2,1)}), bf16[256,512]{1,0:T(8,128)(2,1)}) %reduce-scatter.2.cloned.1.call-update) | async-done | bytes 262160 | tf_op jit(solution)/shard_map/reduce_scatter | solution.py:61
  44.6 1.1 %fusion.19 = (f32[256,512]{1,0:T(8,128)S(1)}, f32[256,512]{1,0:T(8,128)S(1)}) fusion(bf16[256,512]{1,0:T(8,128)(2,1)} %reduce-scatter.2.cloned.1.call-done, f32[256]{0:T(256)S(1)} %convert_element_type.35, f32[256]{0:T(256)S(1)} %convert_element_type.34), kind=kLoop, calls=%fused_computation.30 | loop fusion | flops 655360 | bytes 1312768 | tf_op jit(solution)/shard_map/min | solution.py:25
  45.8 0.7 fusion.11
  46.5 13.2 %psum.7 = f32[256]{0:T(256)S(1)} all-reduce(f32[256]{0:T(256)S(1)} %slice_reduce_fusion), channel_id=1, replica_groups=mesh['year'=8,'port'=4] {'year'}, use_global_device_ids=true, to_apply=%region_2.3 | all-reduce | flops 256 | bytes 2048 | tf_op jit(solution)/shard_map/psum | solution.py:91
  59.7 0.0 copy-done.2
  59.7 0.0 copy-done.3
  59.7 0.0 copy-done.4
  59.7 0.6 maximum_minimum_fusion
  60.4 1.1 %sort.34 = (f32[256,32]{0,1:T(8,128)S(1)}, s32[256,32]{0,1:T(8,128)}) sort(f32[256,32]{0,1:T(8,128)S(1)} %get-tuple-element.107, s32[256,32]{0,1:T(8,128)S(1)} %iota.16), dimensions={1}, to_apply=%region_3.4 | sort | flops 106496 | bytes 131072 | tf_op jit(solution)/shard_map/jit(sort)/sort | solution.py:29
  61.5 8.3 %all-gather = f32[2048,16]{0,1:T(8,128)S(1)} all-gather(f32[256,16]{0,1:T(8,128)S(1)} %slice.54), channel_id=2, replica_groups=mesh['year'=8,'port'=4] {'year'}, dimensions={0}, use_global_device_ids=true | all-gather | bytes 147456 | tf_op jit(solution)/shard_map/all_gather | solution.py:14
  69.8 8.1 %while.15 = (s32[]{:T(128)}, f32[256,16]{0,1:T(8,128)S(1)}, f32[8,256,16]{1,0,2:T(8,128)S(1)}, s32[]{:T(128)}, s32[]{:T(128)}, /*index=5*/s32[]{:T(128)}) while((s32[]{:T(128)}, f32[256,16]{0,1:T(8,128)S(1)}, f32[8,256,16]{1,0,2:T(8,128)S(1)}, s32[]{:T(128)}, s32[]{:T(128)}, /*index=5*/s32[]{:T(128)}) %tuple.56), condition=%wide.region_6.7_spmd, body=%wide.region_4.6_spmd.sunk | while | flops 114693 | bytes 327795 | solution.py:19
  69.9 1.1 %sort.36 = (f32[256,32]{0,1:T(8,128)S(1)}, s32[256,32]{0,1:T(8,128)}) sort(f32[256,32]{0,1:T(8,128)S(1)} %pad_maximum_fusion.2, s32[256,32]{0,1:T(8,128)S(1)} %iota.18), dimensions={1}, to_apply=%region_5.5 | sort | flops 106496 | bytes 131072 | tf_op jit(solution)/shard_map/while/body/eval_jaxpr/jit(sort)/sort | solution.py:29
  71.0 1.1 %sort.36 = (f32[256,32]{0,1:T(8,128)S(1)}, s32[256,32]{0,1:T(8,128)}) sort(f32[256,32]{0,1:T(8,128)S(1)} %pad_maximum_fusion.2, s32[256,32]{0,1:T(8,128)S(1)} %iota.18), dimensions={1}, to_apply=%region_5.5 | sort | flops 106496 | bytes 131072 | tf_op jit(solution)/shard_map/while/body/eval_jaxpr/jit(sort)/sort | solution.py:29
  72.2 1.1 %sort.36 = (f32[256,32]{0,1:T(8,128)S(1)}, s32[256,32]{0,1:T(8,128)}) sort(f32[256,32]{0,1:T(8,128)S(1)} %pad_maximum_fusion.2, s32[256,32]{0,1:T(8,128)S(1)} %iota.18), dimensions={1}, to_apply=%region_5.5 | sort | flops 106496 | bytes 131072 | tf_op jit(solution)/shard_map/while/body/eval_jaxpr/jit(sort)/sort | solution.py:29
  73.3 1.1 %sort.36 = (f32[256,32]{0,1:T(8,128)S(1)}, s32[256,32]{0,1:T(8,128)}) sort(f32[256,32]{0,1:T(8,128)S(1)} %pad_maximum_fusion.2, s32[256,32]{0,1:T(8,128)S(1)} %iota.18), dimensions={1}, to_apply=%region_5.5 | sort | flops 106496 | bytes 131072 | tf_op jit(solution)/shard_map/while/body/eval_jaxpr/jit(sort)/sort | solution.py:29
  74.5 1.1 %sort.36 = (f32[256,32]{0,1:T(8,128)S(1)}, s32[256,32]{0,1:T(8,128)}) sort(f32[256,32]{0,1:T(8,128)S(1)} %pad_maximum_fusion.2, s32[256,32]{0,1:T(8,128)S(1)} %iota.18), dimensions={1}, to_apply=%region_5.5 | sort | flops 106496 | bytes 131072 | tf_op jit(solution)/shard_map/while/body/eval_jaxpr/jit(sort)/sort | solution.py:29
  75.6 1.1 %sort.36 = (f32[256,32]{0,1:T(8,128)S(1)}, s32[256,32]{0,1:T(8,128)}) sort(f32[256,32]{0,1:T(8,128)S(1)} %pad_maximum_fusion.2, s32[256,32]{0,1:T(8,128)S(1)} %iota.18), dimensions={1}, to_apply=%region_5.5 | sort | flops 106496 | bytes 131072 | tf_op jit(solution)/shard_map/while/body/eval_jaxpr/jit(sort)/sort | solution.py:29
  76.8 1.1 %sort.36 = (f32[256,32]{0,1:T(8,128)S(1)}, s32[256,32]{0,1:T(8,128)}) sort(f32[256,32]{0,1:T(8,128)S(1)} %pad_maximum_fusion.2, s32[256,32]{0,1:T(8,128)S(1)} %iota.18), dimensions={1}, to_apply=%region_5.5 | sort | flops 106496 | bytes 131072 | tf_op jit(solution)/shard_map/while/body/eval_jaxpr/jit(sort)/sort | solution.py:29
  77.9 0.6 broadcast_multiply_fusion
  (46 shorter events, 0.3 us)
Async XLA Ops:
  7.2 37.4 %reduce-scatter.2.cloned.1.call-start = ((), (), s32[]{:S(2)}) async-start(), calls=%async_computation.1 | async-start | bytes 1310720 | tf_op jit(solution)/shard_map/reduce_scatter | solution.py:61
  14.4 0.7 copy-start
  14.4 0.7 copy-start.5
  14.4 0.7 copy-start.6
  14.4 0.7 copy-start.1
  15.1 44.5 %copy-start.2 = (f32[256]{0:T(256)S(1)}, f32[256]{0:T(256)}, u32[]{:S(2)}) copy-start(f32[256]{0:T(256)} %param.25) | copy-start | bytes 3076
  15.2 44.5 %copy-start.3 = (f32[256]{0:T(256)S(1)}, f32[256]{0:T(256)}, u32[]{:S(2)}) copy-start(f32[256]{0:T(256)} %param.24) | copy-start | bytes 3076
  15.2 44.5 %copy-start.4 = (f32[256]{0:T(256)S(1)}, f32[256]{0:T(256)}, u32[]{:S(2)}) copy-start(f32[256]{0:T(256)} %param.23) | copy-start | bytes 3076
Sparse Core Ops, SparseCore 0:
  14.6 29.9 reduce-scatter.1
where the time goes:
time: 85.7 us; the launch traced here: 85.3 us
  waiting for transfers between devices  29.4 us (34%)
  blocking collectives  21.5 us (25%)
  between operations  14.1 us (16%)
  other arithmetic  12.1 us (14%)
  matrix products  6.14 us (7%)
  local copies, waits for them, and re-layouts  1.82 us (2%)
    reduce_scatter x1, waiting for transfers between devices, on_device(): lax.psum_scatter(lax.dot_general(weights, ceded_loss, contract, preferred...  29.4 us
    psum x1, blocking collectives, on_device(): summed = lax.psum(jnp.sum(kept_annual, axis=1), 'year')  13.2 us
    sort x8, other arithmetic, top_years(): return jnp.sort(values, axis=1)[:, values.shape[1] - keep_count:]  8.77 us
    all_gather x1, blocking collectives, combined_all(): gathered = lax.all_gather(part, axis)  8.27 us
    dot_general x1, matrix products, on_device(): lax.dot_general(weights, ceded_loss, contract, preferred_element_type=jnp...  5.45 us
    min x2, other arithmetic, clamp_between(): return jnp.minimum(jnp.maximum(values, lower), upper)  1.78 us
  transfers between devices with their start and end apart: 1, of which 1 were waited for; matrix products, arithmetic and copies ran while one was open for 0% of the time, Pallas kernels for 0%

commit v1 on v0

--- a/solution.py
+++ b/solution.py
@@ -8,6 +8,12 @@
 YEAR_DEV = 32
 TAIL = 16
 UNIT_LOSS = 1.0
+
+
+def gather_and_add(array, mesh_axis):
+    shards = lax.all_gather(array, mesh_axis, axis=0, tiled=False)
+    acc = shards.sum(axis=0)
+    return acc
 
 
 def combined_all(part, axis, combine):
@@ -88,7 +94,7 @@
         - reinstate_rate[:, None] * jnp.minimum(layer_paid, (reinstated * limit_loss)[:, None])
     ) / limit_loss[:, None]
     year_total = YEAR_DEV * lax.axis_size("year")
-    summed = lax.psum(jnp.sum(kept_annual, axis=1), "year")
+    summed = gather_and_add(jnp.sum(kept_annual, axis=1), "year")
     base_loss = UNIT_LOSS + summed / year_total
     loss_ratio = kept_annual / base_loss[:, None]
 

time: 85.7 us -> 82.3 us (0.960)
  blocking collectives: 21.5 us -> 18.1 us
    psum x1 -> x0, blocking collectives: 13.2 us -> none  [on_device(): summed = lax.psum(jnp.sum(kept_annual, axis=1), 'year')]
    all_gather x0 -> x1, blocking collectives: none -> 8.9 us  [gather_and_add(): shards = lax.all_gather(array, mesh_axis, axis=0, tiled=False)]
    all_gather x1, blocking collectives: 8.27 us -> 9.17 us  [combined_all(): gathered = lax.all_gather(part, axis)]
where the time goes in v1:
time: 82.3 us; the launch traced here: 81.9 us
  waiting for transfers between devices  29.4 us (36%)
  blocking collectives  18.1 us (22%)
  between operations  14.1 us (17%)
  other arithmetic  12.1 us (15%)
  matrix products  6.14 us (7%)
  local copies, waits for them, and re-layouts  1.82 us (2%)
    reduce_scatter x1, waiting for transfers between devices, on_device(): lax.psum_scatter(lax.dot_general(weights, ceded_loss, contract, preferred...  29.4 us
    all_gather x1, blocking collectives, combined_all(): gathered = lax.all_gather(part, axis)  9.17 us
    all_gather x1, blocking collectives, gather_and_add(): shards = lax.all_gather(array, mesh_axis, axis=0, tiled=False)  8.9 us
    sort x8, other arithmetic, top_years(): return jnp.sort(values, axis=1)[:, values.shape[1] - keep_count:]  8.77 us
    dot_general x1, matrix products, on_device(): lax.dot_general(weights, ceded_loss, contract, preferred_element_type=jnp...  5.45 us
    min x2, other arithmetic, clamp_between(): return jnp.minimum(jnp.maximum(values, lower), upper)  1.78 us
  transfers between devices with their start and end apart: 1, of which 1 were waited for; matrix products, arithmetic and copies ran while one was open for 0% of the time, Pallas kernels for 0%

profile of v1, /device:TPU:0, one launch (start us, length us, event | category | flops | bytes accessed | tf_op | source)
XLA Modules:
  0.0 81.9 jit_solution(17365447736727325406)
XLA Ops:
  7.2 0.0 reduce-scatter.2.cloned.1.call-start
  7.2 0.9 %fusion.23 = (s32[1024,1]{0,1:T(1,128)S(1)}, s32[1024,1]{0,1:T(1,128)S(1)}, s32[1024,1]{0,1:T(1,128)S(1)}, s32[1024,1]{0,1:T(1,128)S(1)}) fusion(s32[1024,4]{0,1:T(4,128)} %param.19), kind=kLoop, calls=%fused_computation.49 | loop fusion | bytes 32768 | tf_op jit(solution)/shard_map/slice | solution.py:59
  8.1 0.9 %slice_convert_fusion.3 = (f32[1024,1]{0,1:T(1,128)S(1)}, f32[1024,1]{0,1:T(1,128)S(1)}, f32[1024,1]{0,1:T(1,128)S(1)}, f32[1024,1]{0,1:T(1,128)S(1)}) fusion(bf16[1024,4]{0,1:T(4,128)(2,1)} %param.18), kind=kLoop, calls=%fused_computation.41 | loop fusion | flops 4096 | bytes 24576 | tf_op jit(solution)/shard_map/jit(_where)/broadcast_in_dim | solution.py:60
  9.0 5.4 %fusion.10 = bf16[1024,512]{1,0:T(8,128)(2,1)} fusion(f32[1024]{0:T(1024)S(1)} %bitcast.28, s32[1024]{0:T(1024)S(1)} %bitcast.24, f32[1024]{0:T(1024)S(1)} %bitcast.29, s32[1024]{0:T(1024)S(1)} %bitcast.25, f32[1024]{0:T(1024)S(1)} %bitcast.27, s32[1024]{0:T(1024)S(1)} %bitcast.23, f32[1024]{0:T(1024)S(1)} %bitcast.26, s32[1024]{0:T(1024)S(1)} %bitcast.22, ...), kind=kOutput, calls=%fused_computation.19 | convolution fusion | flops 1089994752 | bytes 2138112 | tf_op jit(solution)/shard_map/dot_general | solution.py:68
  14.4 0.0 copy-start
  14.4 0.0 copy-start.5
  14.4 0.0 copy-start.6
  14.4 0.0 copy-start.1
  14.4 0.0 reduce-scatter.2.cloned.1.call-update
  14.5 0.6 copy-done
  15.1 0.0 copy-done.5
  15.1 0.0 copy-done.6
  15.1 0.0 copy-done.1
  15.1 0.0 copy-start.2
  15.2 0.0 copy-start.3
  15.2 0.0 copy-start.4
  15.2 29.4 %reduce-scatter.2.cloned.1.call-done = bf16[256,512]{1,0:T(8,128)(2,1)} async-done(((bf16[1024,512]{1,0:T(8,128)(2,1)}), bf16[256,512]{1,0:T(8,128)(2,1)}) %reduce-scatter.2.cloned.1.call-update) | async-done | bytes 262160 | tf_op jit(solution)/shard_map/reduce_scatter | solution.py:67
  44.6 1.1 %fusion.19 = (f32[256,512]{1,0:T(8,128)S(1)}, f32[256,512]{1,0:T(8,128)S(1)}) fusion(bf16[256,512]{1,0:T(8,128)(2,1)} %reduce-scatter.2.cloned.1.call-done, f32[256]{0:T(256)S(1)} %convert_element_type.35, f32[256]{0:T(256)S(1)} %convert_element_type.34), kind=kLoop, calls=%fused_computation.30 | loop fusion | flops 655360 | bytes 1312768 | tf_op jit(solution)/shard_map/min | solution.py:31
  45.8 0.7 fusion.11
  46.5 8.9 %all-gather.2 = f32[8,1,256]{2,1,0:T(1,128)S(1)} all-gather(f32[1,1,256]{2,1,0:T(1,128)S(1)} %bitcast.21), channel_id=2, replica_groups=mesh['year'=8,'port'=4] {'year'}, dimensions={0}, use_global_device_ids=true | all-gather | bytes 9216 | tf_op jit(solution)/shard_map/all_gather | solution.py:14
  55.4 0.0 copy-done.2
  55.4 0.0 copy-done.3
  55.4 0.0 copy-done.4
  55.4 0.6 maximum_minimum_fusion
  56.1 1.1 %sort.34 = (f32[256,32]{0,1:T(8,128)S(1)}, s32[256,32]{0,1:T(8,128)}) sort(f32[256,32]{0,1:T(8,128)S(1)} %get-tuple-element.110, s32[256,32]{0,1:T(8,128)S(1)} %iota.16), dimensions={1}, to_apply=%region_3.4 | sort | flops 106496 | bytes 131072 | tf_op jit(solution)/shard_map/jit(sort)/sort | solution.py:35
  57.2 9.2 %all-gather.1 = f32[2048,16]{0,1:T(8,128)S(1)} all-gather(f32[256,16]{0,1:T(8,128)S(1)} %slice.54), channel_id=3, replica_groups=mesh['year'=8,'port'=4] {'year'}, dimensions={0}, use_global_device_ids=true | all-gather | bytes 147456 | tf_op jit(solution)/shard_map/all_gather | solution.py:20
  66.4 8.1 %while.15 = (s32[]{:T(128)}, f32[256,16]{0,1:T(8,128)S(1)}, f32[8,256,16]{1,0,2:T(8,128)S(1)}, s32[]{:T(128)}, s32[]{:T(128)}, /*index=5*/s32[]{:T(128)}) while((s32[]{:T(128)}, f32[256,16]{0,1:T(8,128)S(1)}, f32[8,256,16]{1,0,2:T(8,128)S(1)}, s32[]{:T(128)}, s32[]{:T(128)}, /*index=5*/s32[]{:T(128)}) %tuple.57), condition=%wide.region_6.7_spmd, body=%wide.region_4.6_spmd.sunk | while | flops 114693 | bytes 327795 | solution.py:25
  66.5 1.1 %sort.36 = (f32[256,32]{0,1:T(8,128)S(1)}, s32[256,32]{0,1:T(8,128)}) sort(f32[256,32]{0,1:T(8,128)S(1)} %pad_maximum_fusion.2, s32[256,32]{0,1:T(8,128)S(1)} %iota.18), dimensions={1}, to_apply=%region_5.5 | sort | flops 106496 | bytes 131072 | tf_op jit(solution)/shard_map/while/body/eval_jaxpr/jit(sort)/sort | solution.py:35
  67.6 1.1 %sort.36 = (f32[256,32]{0,1:T(8,128)S(1)}, s32[256,32]{0,1:T(8,128)}) sort(f32[256,32]{0,1:T(8,128)S(1)} %pad_maximum_fusion.2, s32[256,32]{0,1:T(8,128)S(1)} %iota.18), dimensions={1}, to_apply=%region_5.5 | sort | flops 106496 | bytes 131072 | tf_op jit(solution)/shard_map/while/body/eval_jaxpr/jit(sort)/sort | solution.py:35
  68.8 1.1 %sort.36 = (f32[256,32]{0,1:T(8,128)S(1)}, s32[256,32]{0,1:T(8,128)}) sort(f32[256,32]{0,1:T(8,128)S(1)} %pad_maximum_fusion.2, s32[256,32]{0,1:T(8,128)S(1)} %iota.18), dimensions={1}, to_apply=%region_5.5 | sort | flops 106496 | bytes 131072 | tf_op jit(solution)/shard_map/while/body/eval_jaxpr/jit(sort)/sort | solution.py:35
  69.9 1.1 %sort.36 = (f32[256,32]{0,1:T(8,128)S(1)}, s32[256,32]{0,1:T(8,128)}) sort(f32[256,32]{0,1:T(8,128)S(1)} %pad_maximum_fusion.2, s32[256,32]{0,1:T(8,128)S(1)} %iota.18), dimensions={1}, to_apply=%region_5.5 | sort | flops 106496 | bytes 131072 | tf_op jit(solution)/shard_map/while/body/eval_jaxpr/jit(sort)/sort | solution.py:35
  71.1 1.1 %sort.36 = (f32[256,32]{0,1:T(8,128)S(1)}, s32[256,32]{0,1:T(8,128)}) sort(f32[256,32]{0,1:T(8,128)S(1)} %pad_maximum_fusion.2, s32[256,32]{0,1:T(8,128)S(1)} %iota.18), dimensions={1}, to_apply=%region_5.5 | sort | flops 106496 | bytes 131072 | tf_op jit(solution)/shard_map/while/body/eval_jaxpr/jit(sort)/sort | solution.py:35
  72.2 1.1 %sort.36 = (f32[256,32]{0,1:T(8,128)S(1)}, s32[256,32]{0,1:T(8,128)}) sort(f32[256,32]{0,1:T(8,128)S(1)} %pad_maximum_fusion.2, s32[256,32]{0,1:T(8,128)S(1)} %iota.18), dimensions={1}, to_apply=%region_5.5 | sort | flops 106496 | bytes 131072 | tf_op jit(solution)/shard_map/while/body/eval_jaxpr/jit(sort)/sort | solution.py:35
  73.4 1.1 %sort.36 = (f32[256,32]{0,1:T(8,128)S(1)}, s32[256,32]{0,1:T(8,128)}) sort(f32[256,32]{0,1:T(8,128)S(1)} %pad_maximum_fusion.2, s32[256,32]{0,1:T(8,128)S(1)} %iota.18), dimensions={1}, to_apply=%region_5.5 | sort | flops 106496 | bytes 131072 | tf_op jit(solution)/shard_map/while/body/eval_jaxpr/jit(sort)/sort | solution.py:35
  74.5 0.6 broadcast_multiply_fusion
  (47 shorter events, 0.4 us)
Async XLA Ops:
  7.2 37.4 %reduce-scatter.2.cloned.1.call-start = ((), (), s32[]{:S(2)}) async-start(), calls=%async_computation.1 | async-start | bytes 1310720 | tf_op jit(solution)/shard_map/reduce_scatter | solution.py:67
  14.4 0.7 copy-start
  14.4 0.7 copy-start.5
  14.4 0.7 copy-start.6
  14.4 0.7 copy-start.1
  15.1 40.3 %copy-start.2 = (f32[256]{0:T(256)S(1)}, f32[256]{0:T(256)}, u32[]{:S(2)}) copy-start(f32[256]{0:T(256)} %param.25) | copy-start | bytes 3076
  15.2 40.3 %copy-start.3 = (f32[256]{0:T(256)S(1)}, f32[256]{0:T(256)}, u32[]{:S(2)}) copy-start(f32[256]{0:T(256)} %param.24) | copy-start | bytes 3076
  15.2 40.3 %copy-start.4 = (f32[256]{0:T(256)S(1)}, f32[256]{0:T(256)}, u32[]{:S(2)}) copy-start(f32[256]{0:T(256)} %param.23) | copy-start | bytes 3076
Sparse Core Ops, SparseCore 0:
  14.6 29.9 reduce-scatter.1
